TPU v7x, 128 devices: a whole 4x4x4 slice. The times are simulated.
128 devices in a mesh: blk: 64 (over x, y_lo, z, core), grp: 2 (over y_hi).
Axes of the slice: x: 4, y: 4 (y_hi: 2, y_lo: 2; y = y_hi * 2 + y_lo), z: 4, core: 2. Of those that a mesh axis runs over, the one named last changes fastest.
Arguments:
- left_real: bfloat16 [16384, 8192], P('blk'), may hold values from -6 to 6
- left_imag: bfloat16 [16384, 8192], P('blk'), may hold values from -6 to 6
- right_real: bfloat16 [8192, 512], P('blk', 'grp'), may hold values from -0.0625 to 0.0625
- right_imag: bfloat16 [8192, 512], P('blk', 'grp'), may hold values from -0.0625 to 0.0625
- row_scale: float32 [16384], P('blk'), may hold values from 0.25 to 4
- bond_order: int32 [8192], replicated, may hold values from 0 to 8191, each once
Outputs:
- result_real: float32 [16384, 512], P('blk', 'grp')
- result_imag: float32 [16384, 512], P('blk', 'grp')
Inputs may be any that keep to these rules, and one draw needn't show every extreme that they name: bond_order names each of 0 to 8191 exactly once.
All inputs are finite; a program needn't handle non-finite values.
Results may differ from a plain program's by a relative error of at most 0.0003.
Values may be sent and summed in bfloat16 or wider, within the bound.
A program may use at most 128 MiB of HBM per device.

v0:
```python
import functools

import jax
import jax.numpy as jnp
from jax import lax
from jax.experimental import pallas as pl
from jax.experimental.pallas import tpu as pltpu
from jax.sharding import PartitionSpec as P

MESH = pl.DeviceIdType.MESH
LANES = 128
GROUP = 256
PIECES = 4
STAGES = 8
UNROLL = 16


def kernel(
    devices, groups,
    lr_hbm, li_hbm, rr_ref, ri_ref, scale_ref, order_ref,
    out_r, out_i, factor_ref,
    left_v, table, picked, perm, held, acc,
    left_sem, ring_send, ring_recv, pair_send, pair_recv,
    sums, group_sums, sum_send, sum_recv, group_send, group_recv,
):
    rows, bond = lr_hbm.shape
    depth, cols = rr_ref.shape
    chips = devices // 2
    far = chips // 2
    per = GROUP // LANES
    words = 2 * per
    width = bond // STAGES
    piece = 2 * cols // PIECES

    me = lax.axis_index("blk")
    my_group = lax.axis_index("grp")
    chip, core = me // 2, lax.rem(me, 2)
    other = 1 - core
    place = jnp.where(lax.rem(chip, 2) == 0, chip // 2, chips - 1 - chip // 2)

    def chip_at(p):
        p = lax.rem(p + 2 * chips, chips)
        return jnp.where(p < far, 2 * p, 2 * (chips - 1 - p) + 1)

    def block_at(p, which):
        return chip_at(p) * 2 + which

    partner = chip * 2 + other
    ahead = (block_at(place + 1, core), block_at(place - 1, core))

    def read_left(group, stage):
        return [
            pltpu.make_async_copy(
                src.at[pl.ds(group * GROUP, GROUP), pl.ds(stage * width, width)],
                left_v.at[n, stage],
                left_sem.at[n, stage],
            )
            for n, src in enumerate((lr_hbm, li_hbm))
        ]

    for stage in range(STAGES):
        for copy in read_left(0, stage):
            copy.start()

    barrier = pltpu.get_barrier_semaphore()
    for o in range(1, devices):
        target = lax.rem(me + o, devices)
        pl.semaphore_signal(barrier, inc=1, device_id={"blk": target}, device_id_type=MESH)
    for o in range(1, groups):
        target = lax.rem(my_group + o, groups)
        pl.semaphore_signal(barrier, inc=1, device_id={"grp": target}, device_id_type=MESH)

    for n, ref in enumerate((rr_ref, ri_ref)):
        held[me, n * cols:(n + 1) * cols, :] = (
            ref[...].astype(jnp.float32).T.astype(jnp.bfloat16)
        )
    acc[...] = jnp.zeros_like(acc)
    pl.semaphore_wait(barrier, devices + groups - 2)

    def chunk(block, c):
        return held.at[block, pl.ds(c * piece, piece), :]

    def plan(way):
        full = [(d, c) for d in range(1, far) for c in range(PIECES)]
        half = range(PIECES // 2) if way == 0 else range(PIECES // 2, PIECES)
        return full + [(far, c) for c in half]

    plans = (plan(0), plan(1))
    rounds = len(plans[0])

    def source(way, d):
        return place - d if way == 0 else place + d

    def ring_copy(way, slot, block):
        return pltpu.make_async_remote_copy(
            src_ref=chunk(block, plans[way][slot][1]),
            dst_ref=chunk(block, plans[way][slot][1]),
            send_sem=ring_send.at[way, slot],
            recv_sem=ring_recv.at[way, slot],
            device_id={"blk": ahead[way]},
            device_id_type=MESH,
        )

    def send_ring(way, slot):
        block = block_at(source(way, plans[way][slot][0] - 1), core)
        ring_copy(way, slot, block).start()

    def wait_ring(way, slot):
        block = block_at(source(way, plans[way][slot][0]), core)
        ring_copy(way, slot, block).wait_recv()

    def pair_copy(way, slot, which):
        d, c = (0, slot) if way == 2 else plans[way][slot]
        block = block_at(place if way == 2 else source(way, d), which)
        return pltpu.make_async_remote_copy(
            src_ref=chunk(block, c),
            dst_ref=chunk(block, c),
            send_sem=pair_send.at[way, slot],
            recv_sem=pair_recv.at[way, slot],
            device_id={"blk": partner},
            device_id_type=MESH,
        )

    slot_of = tuple({entry: slot for slot, entry in enumerate(p)} for p in plans)
    for slot in range(PIECES):
        for way in range(2):
            c = slot
            if (1, c) in slot_of[way]:
                send_ring(way, slot_of[way][(1, c)])
    for c in range(PIECES):
        pair_copy(2, c, core).start()

    def pass_on(slot):
        for way in range(2):
            wait_ring(way, slot)
            d, c = plans[way][slot]
            later = slot_of[way].get((d + 1, c))
            if later is not None:
                send_ring(way, later)
            pair_copy(way, slot, core).start()

    def turn(group, stage):
        for copy in read_left(group, stage):
            copy.wait()

        def step(t, _):
            at = pl.multiple_of(t * LANES, LANES)
            for n in range(2):
                for h in range(per):
                    tile = left_v[n, stage, h * LANES:(h + 1) * LANES, pl.ds(at, LANES)]
                    first = pl.multiple_of(stage * width + at, LANES)
                    table[pl.ds(first, LANES), n * per + h, :] = tile.astype(jnp.float32).T
            return 0

        lax.fori_loop(0, width // LANES, step, 0, unroll=2)

    def pick(block):
        base = block * depth

        def step(s, _):
            at = s * UNROLL
            got = []
            for u in range(UNROLL):
                got.append(table[order_ref[base + at + u]])
            for u in range(UNROLL):
                picked[pl.ds(pl.multiple_of((at + u) * words, words), words), :] = got[u]
            return 0

        lax.fori_loop(0, depth // UNROLL, step, 0)
        for w in range(words):
            perm[block, :, w * LANES:(w + 1) * LANES] = picked[
                pl.ds(w, depth, stride=words), :
            ].astype(jnp.bfloat16)

    def multiply(block):
        acc[...] += jnp.dot(held[block], perm[block], preferred_element_type=jnp.float32)

    def multiply_chip(p):
        def step(which, _):
            multiply(block_at(p, which))
            return 0

        lax.fori_loop(0, 2, step, 0)

    def sum_copy(o):
        return pltpu.make_async_remote_copy(
            src_ref=sums.at[me],
            dst_ref=sums.at[me],
            send_sem=sum_send.at[o - 1],
            recv_sem=sum_recv.at[o - 1],
            device_id={"blk": lax.rem(me + o, devices)},
            device_id_type=MESH,
        )

    def sum_wait(o):
        block = lax.rem(me + devices - o, devices)
        pltpu.make_async_remote_copy(
            src_ref=sums.at[block],
            dst_ref=sums.at[block],
            send_sem=sum_send.at[o - 1],
            recv_sem=sum_recv.at[o - 1],
            device_id={"blk": block},
            device_id_type=MESH,
        ).wait_recv()

    def group_copy(o, which):
        return pltpu.make_async_remote_copy(
            src_ref=group_sums.at[which],
            dst_ref=group_sums.at[which],
            send_sem=group_send.at[o - 1],
            recv_sem=group_recv.at[o - 1],
            device_id={"grp": lax.rem(my_group + o, groups)},
            device_id_type=MESH,
        )

    def finish(group):
        low, high = pl.ds(0, cols), pl.ds(cols, cols)
        scale = scale_ref[:, group * GROUP:(group + 1) * GROUP]
        real = (acc[low, 0:GROUP] - acc[high, GROUP:2 * GROUP]) * scale
        imag = (acc[low, GROUP:2 * GROUP] + acc[high, 0:GROUP]) * scale
        squares = jnp.sum(real * real + imag * imag, axis=0, keepdims=True)
        folded = sum(squares[:, h * LANES:(h + 1) * LANES] for h in range(per))
        sums[me] = folded if group == 0 else sums[me] + folded
        out_r[group * GROUP:(group + 1) * GROUP, :] = real.T
        if group == rows // GROUP - 1:
            for o in range(1, devices):
                sum_copy(o).start()
        out_i[group * GROUP:(group + 1) * GROUP, :] = imag.T

    def pick_some(first, last):
        lax.fori_loop(first, last, lambda b, _: (pick(b), 0)[1], 0)

    work = [functools.partial(turn, 0, s) for s in range(STAGES)]
    parts = 8
    edges = [devices * i // parts for i in range(parts + 1)]
    work += [functools.partial(pick_some, a, b) for a, b in zip(edges, edges[1:])]

    def pair_wait(d):
        for way in range(2):
            for slot, entry in enumerate(plans[way]):
                if entry[0] == d:
                    pair_copy(way, slot, other).wait_recv()

    def multiply_own():
        for c in range(PIECES):
            pair_copy(2, c, other).wait_recv()
        multiply_chip(place)

    def multiply_at(d):
        pair_wait(d)

        def step(i, _):
            side, which = i // 2, lax.rem(i, 2)
            multiply(block_at(place - d + 2 * d * side, which))
            return 0

        lax.fori_loop(0, 4 if d < far else 2, step, 0)

    work.append(multiply_own)
    early = max(1, rounds * 5 // 7)
    done = 0
    todo = list(range(1, far + 1))
    for slot in range(rounds):
        until = len(work) if slot >= early else len(work) * (slot + 1) // (early + 1)
        for item in work[done:until]:
            item()
        done = max(done, until)
        if done == len(work) and todo and todo[0] < plans[0][slot][0]:
            multiply_at(todo.pop(0))
        pass_on(slot)
    for d in todo:
        multiply_at(d)
    finish(0)

    for group in range(1, rows // GROUP):
        for stage in range(STAGES):
            for copy in read_left(group, stage):
                copy.start()
        for stage in range(STAGES):
            turn(group, stage)
        pick_some(0, devices)
        acc[...] = jnp.zeros_like(acc)
        lax.fori_loop(0, devices, lambda b, _: (multiply(b), 0)[1], 0)
        finish(group)

    for o in range(1, devices):
        sum_wait(o)
    group_sums[my_group] = jnp.sum(sums[...], axis=0)
    for way in range(2):
        for slot in range(rounds):
            block = block_at(source(way, plans[way][slot][0] - 1), core)
            ring_copy(way, slot, block).wait_send()
            pair_copy(way, slot, core).wait_send()
    for c in range(PIECES):
        pair_copy(2, c, core).wait_send()
    for o in range(1, devices):
        sum_copy(o).wait_send()
    for o in range(1, groups):
        group_copy(o, my_group).start()
    for o in range(1, groups):
        group_copy(o, lax.rem(my_group + groups - o, groups)).wait_recv()
    total = jnp.sum(jnp.sum(group_sums[...], axis=0), axis=1, keepdims=True)
    factor_ref[...] = 1.0 / jnp.sqrt(total / jnp.float32(rows * cols * devices * groups))
    for o in range(1, groups):
        group_copy(o, my_group).wait_send()


def body(devices, groups, left_real, left_imag, right_real, right_imag, row_scale, bond_order):
    rows, bond = left_real.shape
    depth, cols = right_real.shape
    rounds = PIECES * devices // 4
    vmem = pl.BlockSpec(memory_space=pltpu.VMEM)
    far = pl.BlockSpec(memory_space=pl.ANY)
    words = 2 * GROUP // LANES
    out = jax.ShapeDtypeStruct((rows, cols), jnp.float32)
    real, imag, factor = pl.pallas_call(
        functools.partial(kernel, devices, groups),
        out_shape=(out, out, jax.ShapeDtypeStruct((1, 1), jnp.float32)),
        in_specs=[far, far, vmem, vmem, vmem, pl.BlockSpec(memory_space=pltpu.SMEM)],
        out_specs=(vmem, vmem, vmem),
        scratch_shapes=[
            pltpu.VMEM((2, STAGES, GROUP, bond // STAGES), jnp.bfloat16),
            pltpu.VMEM((bond, words, LANES), jnp.float32),
            pltpu.VMEM((depth * words, LANES), jnp.float32),
            pltpu.VMEM((devices, depth, 2 * GROUP), jnp.bfloat16),
            pltpu.VMEM((devices, 2 * cols, depth), jnp.bfloat16),
            pltpu.VMEM((2 * cols, 2 * GROUP), jnp.float32),
            pltpu.SemaphoreType.DMA((2, STAGES)),
            pltpu.SemaphoreType.DMA((2, rounds)),
            pltpu.SemaphoreType.DMA((2, rounds)),
            pltpu.SemaphoreType.DMA((3, rounds)),
            pltpu.SemaphoreType.DMA((3, rounds)),
            pltpu.VMEM((devices, 1, LANES), jnp.float32),
            pltpu.VMEM((groups, 1, LANES), jnp.float32),
            pltpu.SemaphoreType.DMA((devices - 1,)),
            pltpu.SemaphoreType.DMA((devices - 1,)),
            pltpu.SemaphoreType.DMA((groups - 1,)),
            pltpu.SemaphoreType.DMA((groups - 1,)),
        ],
        compiler_params=pltpu.CompilerParams(
            collective_id=0, has_side_effects=True, vmem_limit_bytes=60 * 1024 * 1024
        ),
    )(left_real, left_imag, right_real, right_imag, row_scale.reshape(1, rows), bond_order)
    return real * factor, imag * factor


def solution(mesh):
    in_specs = (P("blk", None), P("blk", None), P("blk", "grp"), P("blk", "grp"), P("blk"), P())
    out_specs = (P("blk", "grp"), P("blk", "grp"))
    return jax.shard_map(
        functools.partial(body, mesh.shape["blk"], mesh.shape["grp"]),
        mesh=mesh, in_specs=in_specs, out_specs=out_specs, check_vma=False,
    )
```

profile of v0, /device:TPU:0, one launch (start us, length us, event | category | flops | bytes accessed | tf_op | source)
XLA Modules:
  0.0 176.8 jit_solution(15535614496134136498)
XLA Ops:
  0.6 173.7 %shard_map.77 = (f32[256,256]{1,0:T(8,128)}, f32[256,256]{1,0:T(8,128)}, f32[1,1]{1,0:T(1,128)}) custom-call(bf16[256,8192]{1,0:T(8,128)(2,1)} %lr_hbm.1, bf16[256,8192]{1,0:T(8,128)(2,1)} %li_hbm.1, bf16[128,256]{1,0:T(8,128)(2,1)} %rr_ref.1, bf16[128,256]{1,0:T(8,128)(2,1)} %ri_ref.1, f32[1,256]{1,0:T(1,128)} %bitcast.2, s32[8192]{0:T(1024)} %order_ref.1), custom_call_target="tpu_custom_call" | custom-call | tf_op jit(solution)/shard_map/pallas_call | solution.py:316
  174.3 2.5 %broadcast_multiply_fusion = (f32[256,256]{1,0:T(8,128)}, f32[256,256]{1,0:T(8,128)}) fusion(f32[256,256]{1,0:T(8,128)} %get-tuple-element.7, f32[]{:T(128)} %bitcast.1, f32[256,256]{1,0:T(8,128)} %get-tuple-element.5), kind=kLoop, calls=%fused_computation | loop fusion | flops 131072 | bytes 1048580 | tf_op jit(solution)/shard_map/mul | solution.py:344
where the time goes:
time: 178 us; the launch traced here: 177 us
  Pallas kernels  174 us (98%)
  other arithmetic  2.49 us (1%)
    pallas_call x1, Pallas kernels, body(): pl.pallas_call(functools.partial(kernel, devices, groups), out_shape=(out...  174 us

commit v1 on v0

v1 whole, which is shorter than its diff:
```python
import functools
import heapq

import jax
import jax.numpy as jnp
from jax import lax
from jax.experimental import pallas as pl
from jax.experimental.pallas import tpu as pltpu
from jax.sharding import PartitionSpec as P

MESH = pl.DeviceIdType.MESH
LANES = 128
HALF = 2
STAGES = 8
UNROLL = 16
TILES = 8
NX, NY, NZ = 4, 2, 4
DO_COMM, DO_TURN, DO_PICK, DO_MM = True, True, True, True
HOP_US, WIRE_US = 2.4, 0.7
START_US = 2.0
SLACK_US = 0.2
TURN_US, PICK_US = 0.08, 0.3

XP, XM, ZP, ZM, YY = range(5)


def plan():
    events = []
    free = [0.0] * 5
    queue = []
    count = 0

    def send(now, link, half, travel, pieces):
        nonlocal count
        start = max(now, free[link])
        free[link] = start + WIRE_US * len(pieces)
        count += 1
        heapq.heappush(queue, (free[link] + HOP_US, count, link, half, travel, pieces))

    def moved(travel, link):
        dx, dy, dz = travel
        return {
            XP: (dx + 1, dy, dz), XM: (dx - 1, dy, dz), YY: (dx, 1, dz),
            ZP: (dx, dy, dz + 1), ZM: (dx, dy, dz - 1),
        }[link]

    rings = {0: ((XP, XM), (ZP, ZM)), 1: ((ZP, ZM), (XP, XM))}

    def onward(link, half, travel, pieces):
        first, second = rings[half]
        out = []
        stage = 0 if link in first else 1 if link == YY else 2 if link in second else -1
        ring = first if stage == 0 else second if stage == 2 else None
        if ring is not None:
            hops = abs(travel[0] if ring[0] == XP else travel[2])
            if hops == 1:
                mine = tuple(p for p in pieces if p == ring.index(link))
                if mine:
                    out.append((link, mine))
        if stage == -1:
            out += [(k, pieces) for k in first]
        if stage <= 0:
            out.append((YY, pieces))
        if stage <= 1:
            out += [(k, pieces) for k in second]
        return out

    own = [[], []]
    for half in (0, 1):
        own[half] = onward(None, half, (0, 0, 0), (0, 1))
    starts = []
    for pair in zip(*own):
        for half, (link, pieces) in enumerate(pair):
            starts.append((half, link, pieces))
    for half, link, pieces in starts:
        send(0.0, link, half, moved((0, 0, 0), link), pieces)
    while queue:
        now, _, link, half, travel, pieces = heapq.heappop(queue)
        follow = onward(link, half, travel, pieces)
        events.append((now, link, half, travel, pieces, follow))
        for k, p in follow:
            send(now, k, half, moved(travel, k), p)
    return starts, events, moved


def kernel(
    devices,
    lr_hbm, li_hbm, rr_ref, ri_ref, scale_ref, order_ref,
    out_r, out_i, total_ref,
    left_v, table, picked, perm, held, acc,
    left_sem, ring_send, ring_recv, pair_send, pair_recv,
    sums, sum_send, sum_recv,
):
    rows, bond = lr_hbm.shape
    depth, cols = rr_ref.shape
    chips = devices // 2
    per = rows // LANES
    words = 2 * per
    width = bond // STAGES
    piece = 2 * cols // (2 * HALF)

    me = lax.axis_index("blk")
    chip, core = me // 2, lax.rem(me, 2)
    other = 1 - core
    z = lax.rem(chip, NZ)
    y = lax.rem(chip // NZ, NY)
    x = chip // (NZ * NY)
    wrap_x = [lax.rem(x + NX - d, NX) for d in range(NX)]
    wrap_z = [lax.rem(z + NZ - d, NZ) for d in range(NZ)]
    flip_y = [y, 1 - y]

    def chip_of(travel):
        dx, dy, dz = travel
        return (wrap_x[dx % NX] * NY + flip_y[dy]) * NZ + wrap_z[dz % NZ]

    ahead = {
        XP: chip_of((-1, 0, 0)) * 2 + core, XM: chip_of((1, 0, 0)) * 2 + core,
        ZP: chip_of((0, 0, -1)) * 2 + core, ZM: chip_of((0, 0, 1)) * 2 + core,
        YY: chip_of((0, 1, 0)) * 2 + core,
    }
    partner = chip * 2 + other

    def read_left(stage):
        return [
            pltpu.make_async_copy(
                src.at[:, pl.ds(stage * width, width)],
                left_v.at[n, stage],
                left_sem.at[n, stage],
            )
            for n, src in enumerate((lr_hbm, li_hbm))
        ]

    for stage in range(STAGES):
        for copy in read_left(stage):
            copy.start()

    barrier = pltpu.get_barrier_semaphore()
    for o in range(1, devices):
        target = lax.rem(me + o, devices)
        pl.semaphore_signal(barrier, inc=1, device_id={"blk": target}, device_id_type=MESH)

    for n, ref in enumerate((rr_ref, ri_ref)):
        held[me, n * cols:(n + 1) * cols, :] = (
            ref[...].astype(jnp.float32).T.astype(jnp.bfloat16)
        )
    acc[...] = jnp.zeros_like(acc)
    pl.semaphore_wait(barrier, devices - 1)

    starts, events, moved = plan()
    slots = {}
    for i, (_, link, half, travel, pieces, _) in enumerate(events):
        slots[(link, half, travel, pieces)] = i

    def part(where, which, half, pieces):
        first = (half * HALF + pieces[0]) * piece
        return held.at[where * 2 + which, pl.ds(first, piece * len(pieces)), :]

    def ring_copy(link, half, travel, pieces, after):
        ref = part(chip_of(travel), core, half, pieces)
        return pltpu.make_async_remote_copy(
            src_ref=ref, dst_ref=ref,
            send_sem=ring_send.at[slots[(link, half, after, pieces)]],
            recv_sem=ring_recv.at[slots[(link, half, after, pieces)]],
            device_id={"blk": ahead[link]}, device_id_type=MESH,
        )

    def pair_copy(event, which):
        if event is None:
            ref, slot = held.at[chip * 2 + which], len(events)
        else:
            _, link, half, travel, pieces, _ = event
            ref = part(chip_of(travel), which, half, pieces)
            slot = slots[(link, half, travel, pieces)]
        return pltpu.make_async_remote_copy(
            src_ref=ref, dst_ref=ref,
            send_sem=pair_send.at[slot], recv_sem=pair_recv.at[slot],
            device_id={"blk": partner}, device_id_type=MESH,
        )

    def begin():
        if not DO_COMM:
            return
        here = (0, 0, 0)
        for half, link, pieces in starts:
            ring_copy(link, half, here, pieces, moved(here, link)).start()
        pair_copy(None, core).start()

    def arrive(event):
        if not DO_COMM:
            return
        _, link, half, travel, pieces, follow = event
        ring_copy(link, half, travel, pieces, travel).wait_recv()
        for k, p in follow:
            ring_copy(k, half, travel, p, moved(travel, k)).start()
        pair_copy(event, core).start()

    def turn(stage):
        for copy in read_left(stage):
            copy.wait()

    def turn_tiles(stage, first, last):
        if not DO_TURN:
            return

        def step(t, _):
            at = pl.multiple_of(t * LANES, LANES)
            for n in range(2):
                for h in range(per):
                    tile = left_v[n, stage, h * LANES:(h + 1) * LANES, pl.ds(at, LANES)]
                    row = pl.multiple_of(stage * width + at, LANES)
                    table[pl.ds(row, LANES), n * per + h, :] = tile.astype(jnp.float32).T
            return 0

        lax.fori_loop(first, last, step, 0, unroll=2)

    def pick(block):
        if not DO_PICK:
            return
        base = block * depth

        def step(s, _):
            at = s * UNROLL
            got = []
            for u in range(UNROLL):
                got.append(table[order_ref[base + at + u]])
            for u in range(UNROLL):
                picked[pl.ds(pl.multiple_of((at + u) * words, words), words), :] = got[u]
            return 0

        lax.fori_loop(0, depth // UNROLL, step, 0)
        for w in range(words):
            perm[block, :, w * LANES:(w + 1) * LANES] = picked[
                pl.ds(w, depth, stride=words), :
            ].astype(jnp.bfloat16)

    def pick_some(first, last):
        lax.fori_loop(first, last, lambda b, _: (pick(b), 0)[1], 0)

    work = []
    for stage in range(STAGES):
        work.append((0.0, functools.partial(turn, stage)))
        for t in range(0, width // LANES, TILES):
            work.append((TILES * TURN_US, functools.partial(turn_tiles, stage, t, t + TILES)))
    for b in range(0, devices, 8):
        work.append((8 * PICK_US, functools.partial(pick_some, b, b + 8)))

    begin()
    now = 0.0
    todo = list(events)
    for cost, item in work:
        while todo and todo[0][0] + SLACK_US <= now:
            arrive(todo.pop(0))
        item()
        now += cost
    for event in todo:
        arrive(event)
    if DO_COMM:
        for event in [None, *events]:
            pair_copy(event, other).wait_recv()

    def multiply(b, _):
        acc[...] += jnp.dot(held[b], perm[b], preferred_element_type=jnp.float32)
        return 0

    if DO_MM:
        lax.fori_loop(0, devices, multiply, 0)

    low, high = pl.ds(0, cols), pl.ds(cols, cols)
    scale = scale_ref[...]
    real = (acc[low, 0:rows] - acc[high, rows:2 * rows]) * scale
    imag = (acc[low, rows:2 * rows] + acc[high, 0:rows]) * scale
    squares = jnp.sum(real * real + imag * imag, axis=0, keepdims=True)
    sums[me] = sum(squares[:, h * LANES:(h + 1) * LANES] for h in range(per))
    out_r[...] = real.T

    def sum_copy(o):
        return pltpu.make_async_remote_copy(
            src_ref=sums.at[me], dst_ref=sums.at[me],
            send_sem=sum_send.at[o - 1], recv_sem=sum_recv.at[o - 1],
            device_id={"blk": lax.rem(me + o, devices)}, device_id_type=MESH,
        )

    if DO_COMM:
        for o in range(1, devices):
            sum_copy(o).start()
    out_i[...] = imag.T
    if DO_COMM:
        def sum_wait(o):
            block = lax.rem(me + devices - o, devices)
            pltpu.make_async_remote_copy(
                src_ref=sums.at[block], dst_ref=sums.at[block],
                send_sem=sum_send.at[o - 1], recv_sem=sum_recv.at[o - 1],
                device_id={"blk": block}, device_id_type=MESH,
            ).wait()

        for o in range(1, devices):
            sum_wait(o)
    total_ref[...] = jnp.sum(jnp.sum(sums[...], axis=0), axis=1, keepdims=True)
    if DO_COMM:
        here = (0, 0, 0)
        for half, link, pieces in starts:
            ring_copy(link, half, here, pieces, moved(here, link)).wait_send()
        for _, _, half, travel, _, follow in events:
            for k, p in follow:
                ring_copy(k, half, travel, p, moved(travel, k)).wait_send()
        for event in [None, *events]:
            pair_copy(event, core).wait_send()


def body(devices, groups, left_real, left_imag, right_real, right_imag, row_scale, bond_order):
    rows, bond = left_real.shape
    depth, cols = right_real.shape
    messages = len(plan()[1])
    vmem = pl.BlockSpec(memory_space=pltpu.VMEM)
    far = pl.BlockSpec(memory_space=pl.ANY)
    words = 2 * rows // LANES
    out = jax.ShapeDtypeStruct((rows, cols), jnp.float32)
    real, imag, total = pl.pallas_call(
        functools.partial(kernel, devices),
        out_shape=(out, out, jax.ShapeDtypeStruct((1, 1), jnp.float32)),
        in_specs=[far, far, vmem, vmem, vmem, pl.BlockSpec(memory_space=pltpu.SMEM)],
        out_specs=(vmem, vmem, vmem),
        scratch_shapes=[
            pltpu.VMEM((2, STAGES, rows, bond // STAGES), jnp.bfloat16),
            pltpu.VMEM((bond, words, LANES), jnp.float32),
            pltpu.VMEM((depth * words, LANES), jnp.float32),
            pltpu.VMEM((devices, depth, 2 * rows), jnp.bfloat16),
            pltpu.VMEM((devices, 2 * cols, depth), jnp.bfloat16),
            pltpu.VMEM((2 * cols, 2 * rows), jnp.float32),
            pltpu.SemaphoreType.DMA((2, STAGES)),
            pltpu.SemaphoreType.DMA((messages,)),
            pltpu.SemaphoreType.DMA((messages,)),
            pltpu.SemaphoreType.DMA((messages + 1,)),
            pltpu.SemaphoreType.DMA((messages + 1,)),
            pltpu.VMEM((devices, 1, LANES), jnp.float32),
            pltpu.SemaphoreType.DMA((devices - 1,)),
            pltpu.SemaphoreType.DMA((devices - 1,)),
        ],
        compiler_params=pltpu.CompilerParams(
            collective_id=0, has_side_effects=True, vmem_limit_bytes=60 * 1024 * 1024
        ),
    )(left_real, left_imag, right_real, right_imag, row_scale.reshape(1, rows), bond_order)
    whole = total
    for o in range(1, groups):
        ring = [(g, (g + o) % groups) for g in range(groups)]
        whole = whole + lax.ppermute(total, "grp", ring)
    factor = 1.0 / jnp.sqrt(whole / jnp.float32(rows * cols * devices * groups))
    return real * factor, imag * factor


def solution(mesh):
    in_specs = (P("blk", None), P("blk", None), P("blk", "grp"), P("blk", "grp"), P("blk"), P())
    out_specs = (P("blk", "grp"), P("blk", "grp"))
    return jax.shard_map(
        functools.partial(body, mesh.shape["blk"], mesh.shape["grp"]),
        mesh=mesh, in_specs=in_specs, out_specs=out_specs, check_vma=False,
    )
```

time: 178 us -> 78.7 us (0.44)
  Pallas kernels: 174 us -> 69.4 us
  starting transfers between devices: 0 us -> 3.25 us
  waiting for transfers between devices: 0 us -> 2.08 us
    pallas_call x1, Pallas kernels: 174 us -> 69.4 us  [body(): pl.pallas_call(functools.partial(kernel, devices), out_shape=(out, out, j...]
    ppermute x0 -> x1, starting transfers between devices: none -> 3.25 us  [body(): whole = whole + lax.ppermute(total, 'grp', ring)]
    ppermute x0 -> x1, waiting for transfers between devices: none -> 2.08 us  [body(): whole = whole + lax.ppermute(total, 'grp', ring)]
  transfers between devices with their start and end apart: 0 -> 1, of which waited for: 0 -> 1; matrix products, arithmetic and copies ran while one was open for 0% -> 0% of each run, Pallas kernels for 0% -> 0%
where the time goes in v1:
time: 78.7 us; the launch traced here: 78.4 us
  Pallas kernels  69.4 us (88%)
  starting transfers between devices  3.25 us (4%)
  waiting for transfers between devices  2.08 us (3%)
  other arithmetic  1.86 us (2%)
  between operations  1.85 us (2%)
    pallas_call x1, Pallas kernels, body(): pl.pallas_call(functools.partial(kernel, devices), out_shape=(out, out, j...  69.4 us
    ppermute x1, starting transfers between devices, body(): whole = whole + lax.ppermute(total, 'grp', ring)  3.25 us
    ppermute x1, waiting for transfers between devices, body(): whole = whole + lax.ppermute(total, 'grp', ring)  2.08 us
    mul x1, other arithmetic, body(): return (real * factor, imag * factor)  1.86 us
  transfers between devices with their start and end apart: 1, of which 1 were waited for; matrix products, arithmetic and copies ran while one was open for 0% of the time, Pallas kernels for 0%

profile of v1, /device:TPU:0, one launch (start us, length us, event | category | flops | bytes accessed | tf_op | source)
XLA Modules:
  0.0 78.4 jit_solution(1714764507193777239)
XLA Ops:
  0.6 69.4 %shard_map.77 = (f32[256,256]{1,0:T(8,128)}, f32[256,256]{1,0:T(8,128)}, f32[1,1]{1,0:T(1,128)}) custom-call(bf16[256,8192]{1,0:T(8,128)(2,1)} %lr_hbm.1, bf16[256,8192]{1,0:T(8,128)(2,1)} %li_hbm.1, bf16[128,256]{1,0:T(8,128)(2,1)} %rr_ref.1, bf16[128,256]{1,0:T(8,128)(2,1)} %ri_ref.1, f32[1,256]{1,0:T(1,128)} %bitcast.2, s32[8192]{0:T(1024)} %order_ref.1), custom_call_target="tpu_custom_call" | custom-call | tf_op jit(solution)/shard_map/pallas_call | solution.py:318
  70.0 3.2 %collective-permute-start = (f32[1,1]{1,0:T(1,128)}, f32[1,1]{1,0:T(1,128)}, u32[]{:S(2)}, u32[]{:S(2)}) collective-permute-start(f32[1,1]{1,0:T(1,128)} %get-tuple-element.6), channel_id=1, source_target_pairs={{0,1},{1,0},{2,3},{3,2},{4,5},{5,4},{6,7},{7,6},{8,9},{9,8},{10,11... | collective-permute-start | bytes 20 | tf_op jit(solution)/shard_map/ppermute | solution.py:346
  73.3 2.1 %collective-permute-done = f32[1,1]{1,0:T(1,128)} collective-permute-done((f32[1,1]{1,0:T(1,128)}, f32[1,1]{1,0:T(1,128)}, u32[]{:S(2)}, u32[]{:S(2)}) %collective-permute-start) | collective-permute-done | bytes 36 | tf_op jit(solution)/shard_map/ppermute | solution.py:346
  76.6 1.9 %broadcast_multiply_fusion = (f32[256,256]{1,0:T(8,128)}, f32[256,256]{1,0:T(8,128)}) fusion(f32[256,256]{1,0:T(8,128)} %get-tuple-element.7, f32[]{:T(128)} %bitcast.1, f32[256,256]{1,0:T(8,128)} %get-tuple-element.5), kind=kLoop, calls=%fused_computation | loop fusion | flops 131072 | bytes 1048580 | tf_op jit(solution)/shard_map/mul | solution.py:348
Async XLA Ops:
  70.0 5.3 %collective-permute-start = (f32[1,1]{1,0:T(1,128)}, f32[1,1]{1,0:T(1,128)}, u32[]{:S(2)}, u32[]{:S(2)}) collective-permute-start(f32[1,1]{1,0:T(1,128)} %get-tuple-element.6), channel_id=1, source_target_pairs={{0,1},{1,0},{2,3},{3,2},{4,5},{5,4},{6,7},{7,6},{8,9},{9,8},{10,11... | collective-permute-start | bytes 20 | tf_op jit(solution)/shard_map/ppermute | solution.py:346

commit v2 on v1

--- a/solution.py
+++ b/solution.py
@@ -14,12 +14,14 @@
 STAGES = 8
 UNROLL = 16
 TILES = 8
+RUN = 8
 NX, NY, NZ = 4, 2, 4
 DO_COMM, DO_TURN, DO_PICK, DO_MM = True, True, True, True
 HOP_US, WIRE_US = 2.4, 0.7
 START_US = 2.0
 SLACK_US = 0.2
-TURN_US, PICK_US = 0.08, 0.3
+TURN_US, PICK_US = 0.18, 0.18
+MULTIPLY_US, PAIR_US = 0.7, 1.2
 
 XP, XM, ZP, ZM, YY = range(5)
 
@@ -159,21 +161,23 @@
         ref = part(chip_of(travel), core, half, pieces)
         return pltpu.make_async_remote_copy(
             src_ref=ref, dst_ref=ref,
-            send_sem=ring_send.at[slots[(link, half, after, pieces)]],
+            send_sem=ring_send,
             recv_sem=ring_recv.at[slots[(link, half, after, pieces)]],
             device_id={"blk": ahead[link]}, device_id_type=MESH,
         )
 
-    def pair_copy(event, which):
-        if event is None:
-            ref, slot = held.at[chip * 2 + which], len(events)
-        else:
-            _, link, half, travel, pieces, _ = event
-            ref = part(chip_of(travel), which, half, pieces)
-            slot = slots[(link, half, travel, pieces)]
+    batch = 4
+    needs = {}
+    for event in events:
+        dx, dy, dz = event[3]
+        needs.setdefault((dx % NX, dy, dz % NZ), []).append(event)
+    near = sorted(needs, key=lambda k: max(e[0] for e in needs[k]))
+    near = [(0, 0, 0), *near]
+    turn_of = {t: i // batch for i, t in enumerate(near)}
+
+    def pair_copy(ref, slot):
         return pltpu.make_async_remote_copy(
-            src_ref=ref, dst_ref=ref,
-            send_sem=pair_send.at[slot], recv_sem=pair_recv.at[slot],
+            src_ref=ref, dst_ref=ref, send_sem=pair_send, recv_sem=pair_recv.at[slot],
             device_id={"blk": partner}, device_id_type=MESH,
         )
 
@@ -183,7 +187,7 @@
         here = (0, 0, 0)
         for half, link, pieces in starts:
             ring_copy(link, half, here, pieces, moved(here, link)).start()
-        pair_copy(None, core).start()
+        pair_copy(held.at[me], 0).start()
 
     def arrive(event):
         if not DO_COMM:
@@ -192,7 +196,8 @@
         ring_copy(link, half, travel, pieces, travel).wait_recv()
         for k, p in follow:
             ring_copy(k, half, travel, p, moved(travel, k)).start()
-        pair_copy(event, core).start()
+        dx, dy, dz = travel
+        pair_copy(part(chip_of(travel), core, half, pieces), turn_of[(dx % NX, dy, dz % NZ)]).start()
 
     def turn(stage):
         for copy in read_left(stage):
@@ -213,98 +218,110 @@
 
         lax.fori_loop(first, last, step, 0, unroll=2)
 
-    def pick(block):
+    def pick_some(first):
         if not DO_PICK:
             return
-        base = block * depth
-
-        def step(s, _):
-            at = s * UNROLL
-            got = []
-            for u in range(UNROLL):
-                got.append(table[order_ref[base + at + u]])
+        base = first * depth
+        count = RUN * depth
+
+        def fetch(at):
+            return tuple(table[order_ref[base + at + u]] for u in range(UNROLL))
+
+        def put(at, got):
             for u in range(UNROLL):
                 picked[pl.ds(pl.multiple_of((at + u) * words, words), words), :] = got[u]
+
+        def step(s, got):
+            later = fetch(s * UNROLL)
+            put(jnp.maximum(s - 1, 0) * UNROLL, got)
+            return later
+
+        blank = (jnp.zeros((words, LANES), jnp.float32),) * UNROLL
+        put(count - UNROLL, lax.fori_loop(0, count // UNROLL, step, blank))
+
+        def pack(i, _):
+            for w in range(words):
+                perm[first + i, :, w * LANES:(w + 1) * LANES] = picked[
+                    pl.ds(i * depth * words + w, depth, stride=words), :
+                ].astype(jnp.bfloat16)
             return 0
 
-        lax.fori_loop(0, depth // UNROLL, step, 0)
-        for w in range(words):
-            perm[block, :, w * LANES:(w + 1) * LANES] = picked[
-                pl.ds(w, depth, stride=words), :
-            ].astype(jnp.bfloat16)
-
-    def pick_some(first, last):
-        lax.fori_loop(first, last, lambda b, _: (pick(b), 0)[1], 0)
+        lax.fori_loop(0, RUN, pack, 0)
 
     work = []
     for stage in range(STAGES):
         work.append((0.0, functools.partial(turn, stage)))
         for t in range(0, width // LANES, TILES):
             work.append((TILES * TURN_US, functools.partial(turn_tiles, stage, t, t + TILES)))
-    for b in range(0, devices, 8):
-        work.append((8 * PICK_US, functools.partial(pick_some, b, b + 8)))
+    for b in range(0, devices, RUN):
+        work.append((RUN * PICK_US, functools.partial(pick_some, b)))
+
+    def multiply(which):
+        def step(_, carry):
+            blocks = [chip_of(t) * 2 + w for t in which for w in range(2)]
+            lhs = jnp.concatenate([held[b] for b in blocks], axis=1)
+            rhs = jnp.concatenate([perm[b] for b in blocks], axis=0)
+            acc[...] += jnp.dot(lhs, rhs, preferred_element_type=jnp.float32)
+            return carry
+
+        if DO_COMM:
+            pair_copy(held.at[pl.ds(0, len(which))], turn_of[which[0]]).wait_recv()
+        if DO_MM:
+            lax.fori_loop(0, 1, step, 0)
 
     begin()
     now = 0.0
     todo = list(events)
-    for cost, item in work:
+    for first in range(0, chips, batch):
+        which = near[first:first + batch]
+        ready = max([e[0] for t in which for e in needs.get(t, [])])
+        work.append((MULTIPLY_US, functools.partial(multiply, which), ready + PAIR_US))
+    for cost, item, *ready in work:
+        now = max([now, *ready])
         while todo and todo[0][0] + SLACK_US <= now:
             arrive(todo.pop(0))
         item()
         now += cost
-    for event in todo:
-        arrive(event)
-    if DO_COMM:
-        for event in [None, *events]:
-            pair_copy(event, other).wait_recv()
-
-    def multiply(b, _):
-        acc[...] += jnp.dot(held[b], perm[b], preferred_element_type=jnp.float32)
-        return 0
-
-    if DO_MM:
-        lax.fori_loop(0, devices, multiply, 0)
-
+    assert not todo
+
+    total_devices = devices
+    mine = me
     low, high = pl.ds(0, cols), pl.ds(cols, cols)
     scale = scale_ref[...]
     real = (acc[low, 0:rows] - acc[high, rows:2 * rows]) * scale
     imag = (acc[low, rows:2 * rows] + acc[high, 0:rows]) * scale
     squares = jnp.sum(real * real + imag * imag, axis=0, keepdims=True)
-    sums[me] = sum(squares[:, h * LANES:(h + 1) * LANES] for h in range(per))
+    sums[mine] = sum(squares[:, h * LANES:(h + 1) * LANES] for h in range(per))
     out_r[...] = real.T
 
-    def sum_copy(o):
+    def sum_copy(o, which):
+        to = lax.rem(mine + o, total_devices)
         return pltpu.make_async_remote_copy(
-            src_ref=sums.at[me], dst_ref=sums.at[me],
-            send_sem=sum_send.at[o - 1], recv_sem=sum_recv.at[o - 1],
-            device_id={"blk": lax.rem(me + o, devices)}, device_id_type=MESH,
+            src_ref=sums.at[which], dst_ref=sums.at[which],
+            send_sem=sum_send, recv_sem=sum_recv,
+            device_id={"blk": to}, device_id_type=MESH,
         )
 
     if DO_COMM:
-        for o in range(1, devices):
-            sum_copy(o).start()
+        for o in range(1, total_devices):
+            sum_copy(o, mine).start()
     out_i[...] = imag.T
     if DO_COMM:
-        def sum_wait(o):
-            block = lax.rem(me + devices - o, devices)
-            pltpu.make_async_remote_copy(
-                src_ref=sums.at[block], dst_ref=sums.at[block],
-                send_sem=sum_send.at[o - 1], recv_sem=sum_recv.at[o - 1],
-                device_id={"blk": block}, device_id_type=MESH,
-            ).wait()
-
-        for o in range(1, devices):
-            sum_wait(o)
+        sent = held.at[pl.ds(0, chips - 1)]
+        pltpu.make_async_remote_copy(
+            src_ref=sent, dst_ref=sent, send_sem=ring_send, recv_sem=sum_recv,
+            device_id={"blk": partner}, device_id_type=MESH,
+        ).wait_send()
+        pair_copy(held.at[pl.ds(0, chips)], 0).wait_send()
+        others = sums.at[pl.ds(0, total_devices - 1)]
+        exchange = pltpu.make_async_remote_copy(
+            src_ref=others, dst_ref=others, send_sem=sum_send, recv_sem=sum_recv,
+            device_id={"blk": partner}, device_id_type=MESH,
+        )
+        exchange.wait_recv()
     total_ref[...] = jnp.sum(jnp.sum(sums[...], axis=0), axis=1, keepdims=True)
     if DO_COMM:
-        here = (0, 0, 0)
-        for half, link, pieces in starts:
-            ring_copy(link, half, here, pieces, moved(here, link)).wait_send()
-        for _, _, half, travel, _, follow in events:
-            for k, p in follow:
-                ring_copy(k, half, travel, p, moved(travel, k)).wait_send()
-        for event in [None, *events]:
-            pair_copy(event, core).wait_send()
+        exchange.wait_send()
 
 
 def body(devices, groups, left_real, left_imag, right_real, right_imag, row_scale, bond_order):
@@ -323,18 +340,18 @@
         scratch_shapes=[
             pltpu.VMEM((2, STAGES, rows, bond // STAGES), jnp.bfloat16),
             pltpu.VMEM((bond, words, LANES), jnp.float32),
-            pltpu.VMEM((depth * words, LANES), jnp.float32),
+            pltpu.VMEM((RUN * depth * words, LANES), jnp.float32),
             pltpu.VMEM((devices, depth, 2 * rows), jnp.bfloat16),
             pltpu.VMEM((devices, 2 * cols, depth), jnp.bfloat16),
             pltpu.VMEM((2 * cols, 2 * rows), jnp.float32),
             pltpu.SemaphoreType.DMA((2, STAGES)),
+            pltpu.SemaphoreType.DMA,
             pltpu.SemaphoreType.DMA((messages,)),
-            pltpu.SemaphoreType.DMA((messages,)),
-            pltpu.SemaphoreType.DMA((messages + 1,)),
-            pltpu.SemaphoreType.DMA((messages + 1,)),
+            pltpu.SemaphoreType.DMA,
+            pltpu.SemaphoreType.DMA((8,)),
             pltpu.VMEM((devices, 1, LANES), jnp.float32),
-            pltpu.SemaphoreType.DMA((devices - 1,)),
-            pltpu.SemaphoreType.DMA((devices - 1,)),
+            pltpu.SemaphoreType.DMA,
+            pltpu.SemaphoreType.DMA,
         ],
         compiler_params=pltpu.CompilerParams(
             collective_id=0, has_side_effects=True, vmem_limit_bytes=60 * 1024 * 1024

time: 78.7 us -> 58.7 us (0.75)
  Pallas kernels: 69.4 us -> 49.4 us
    pallas_call x1, Pallas kernels: 69.4 us -> 49.4 us  [body(): pl.pallas_call(functools.partial(kernel, devices), out_shape=(out, out, j...]
where the time goes in v2:
time: 58.7 us; the launch traced here: 58.4 us
  Pallas kernels  49.4 us (84%)
  starting transfers between devices  3.25 us (6%)
  waiting for transfers between devices  2.08 us (4%)
  other arithmetic  1.86 us (3%)
  between operations  1.85 us (3%)
    pallas_call x1, Pallas kernels, body(): pl.pallas_call(functools.partial(kernel, devices), out_shape=(out, out, j...  49.4 us
    ppermute x1, starting transfers between devices, body(): whole = whole + lax.ppermute(total, 'grp', ring)  3.25 us
    ppermute x1, waiting for transfers between devices, body(): whole = whole + lax.ppermute(total, 'grp', ring)  2.08 us
    mul x1, other arithmetic, body(): return (real * factor, imag * factor)  1.86 us
  transfers between devices with their start and end apart: 1, of which 1 were waited for; matrix products, arithmetic and copies ran while one was open for 0% of the time, Pallas kernels for 0%

profile of v2, /device:TPU:0, one launch (start us, length us, event | category | flops | bytes accessed | tf_op | source)
XLA Modules:
  0.0 58.4 jit_solution(16581381601395390298)
XLA Ops:
  0.6 49.4 %shard_map.77 = (f32[256,256]{1,0:T(8,128)}, f32[256,256]{1,0:T(8,128)}, f32[1,1]{1,0:T(1,128)}) custom-call(bf16[256,8192]{1,0:T(8,128)(2,1)} %lr_hbm.1, bf16[256,8192]{1,0:T(8,128)(2,1)} %li_hbm.1, bf16[128,256]{1,0:T(8,128)(2,1)} %rr_ref.1, bf16[128,256]{1,0:T(8,128)(2,1)} %ri_ref.1, f32[1,256]{1,0:T(1,128)} %bitcast.2, s32[8192]{0:T(1024)} %order_ref.1), custom_call_target="tpu_custom_call" | custom-call | tf_op jit(solution)/shard_map/pallas_call | solution.py:335
  50.0 3.2 %collective-permute-start = (f32[1,1]{1,0:T(1,128)}, f32[1,1]{1,0:T(1,128)}, u32[]{:S(2)}, u32[]{:S(2)}) collective-permute-start(f32[1,1]{1,0:T(1,128)} %get-tuple-element.6), channel_id=1, source_target_pairs={{0,1},{1,0},{2,3},{3,2},{4,5},{5,4},{6,7},{7,6},{8,9},{9,8},{10,11... | collective-permute-start | bytes 20 | tf_op jit(solution)/shard_map/ppermute | solution.py:363
  53.3 2.1 %collective-permute-done = f32[1,1]{1,0:T(1,128)} collective-permute-done((f32[1,1]{1,0:T(1,128)}, f32[1,1]{1,0:T(1,128)}, u32[]{:S(2)}, u32[]{:S(2)}) %collective-permute-start) | collective-permute-done | bytes 36 | tf_op jit(solution)/shard_map/ppermute | solution.py:363
  56.6 1.9 %broadcast_multiply_fusion = (f32[256,256]{1,0:T(8,128)}, f32[256,256]{1,0:T(8,128)}) fusion(f32[256,256]{1,0:T(8,128)} %get-tuple-element.7, f32[]{:T(128)} %bitcast.1, f32[256,256]{1,0:T(8,128)} %get-tuple-element.5), kind=kLoop, calls=%fused_computation | loop fusion | flops 131072 | bytes 1048580 | tf_op jit(solution)/shard_map/mul | solution.py:365
Async XLA Ops:
  50.0 5.3 %collective-permute-start = (f32[1,1]{1,0:T(1,128)}, f32[1,1]{1,0:T(1,128)}, u32[]{:S(2)}, u32[]{:S(2)}) collective-permute-start(f32[1,1]{1,0:T(1,128)} %get-tuple-element.6), channel_id=1, source_target_pairs={{0,1},{1,0},{2,3},{3,2},{4,5},{5,4},{6,7},{7,6},{8,9},{9,8},{10,11... | collective-permute-start | bytes 20 | tf_op jit(solution)/shard_map/ppermute | solution.py:363

commit v3 on v2

--- a/solution.py
+++ b/solution.py
@@ -20,7 +20,7 @@
 HOP_US, WIRE_US = 2.4, 0.7
 START_US = 2.0
 SLACK_US = 0.2
-TURN_US, PICK_US = 0.18, 0.18
+TURN_US, PICK_US = 0.08, 0.18
 MULTIPLY_US, PAIR_US = 0.7, 1.2
 
 XP, XM, ZP, ZM, YY = range(5)
@@ -137,8 +137,7 @@
             copy.start()
 
     barrier = pltpu.get_barrier_semaphore()
-    for o in range(1, devices):
-        target = lax.rem(me + o, devices)
+    for target in (*ahead.values(), partner):
         pl.semaphore_signal(barrier, inc=1, device_id={"blk": target}, device_id_type=MESH)
 
     for n, ref in enumerate((rr_ref, ri_ref)):
@@ -146,7 +145,7 @@
             ref[...].astype(jnp.float32).T.astype(jnp.bfloat16)
         )
     acc[...] = jnp.zeros_like(acc)
-    pl.semaphore_wait(barrier, devices - 1)
+    pl.semaphore_wait(barrier, len(ahead) + 1)
 
     starts, events, moved = plan()
     slots = {}
@@ -203,6 +202,8 @@
         for copy in read_left(stage):
             copy.wait()
 
+    flat = table.reshape(bond * words, LANES)
+
     def turn_tiles(stage, first, last):
         if not DO_TURN:
             return
@@ -212,8 +213,8 @@
             for n in range(2):
                 for h in range(per):
                     tile = left_v[n, stage, h * LANES:(h + 1) * LANES, pl.ds(at, LANES)]
-                    row = pl.multiple_of(stage * width + at, LANES)
-                    table[pl.ds(row, LANES), n * per + h, :] = tile.astype(jnp.float32).T
+                    row = pl.multiple_of((stage * width + at) * words, LANES) + n * per + h
+                    flat[pl.ds(row, LANES, stride=words), :] = tile.astype(jnp.float32).T
             return 0
 
         lax.fori_loop(first, last, step, 0, unroll=2)

time: 58.7 us -> 52.3 us (0.89)
  Pallas kernels: 49.4 us -> 43.1 us
    pallas_call x1, Pallas kernels: 49.4 us -> 43.1 us  [body(): pl.pallas_call(functools.partial(kernel, devices), out_shape=(out, out, j...]
where the time goes in v3:
time: 52.3 us; the launch traced here: 52.1 us
  Pallas kernels  43.1 us (82%)
  starting transfers between devices  2.98 us (6%)
  waiting for transfers between devices  2.34 us (4%)
  other arithmetic  1.86 us (4%)
  between operations  1.85 us (4%)
    pallas_call x1, Pallas kernels, body(): pl.pallas_call(functools.partial(kernel, devices), out_shape=(out, out, j...  43.1 us
    ppermute x1, starting transfers between devices, body(): whole = whole + lax.ppermute(total, 'grp', ring)  2.98 us
    ppermute x1, waiting for transfers between devices, body(): whole = whole + lax.ppermute(total, 'grp', ring)  2.34 us
    mul x1, other arithmetic, body(): return (real * factor, imag * factor)  1.86 us
  transfers between devices with their start and end apart: 1, of which 1 were waited for; matrix products, arithmetic and copies ran while one was open for 0% of the time, Pallas kernels for 0%

profile of v3, /device:TPU:0, one launch (start us, length us, event | category | flops | bytes accessed | tf_op | source)
XLA Modules:
  0.0 52.1 jit_solution(1895401701274073747)
XLA Ops:
  0.6 43.1 %shard_map.77 = (f32[256,256]{1,0:T(8,128)}, f32[256,256]{1,0:T(8,128)}, f32[1,1]{1,0:T(1,128)}) custom-call(bf16[256,8192]{1,0:T(8,128)(2,1)} %lr_hbm.1, bf16[256,8192]{1,0:T(8,128)(2,1)} %li_hbm.1, bf16[128,256]{1,0:T(8,128)(2,1)} %rr_ref.1, bf16[128,256]{1,0:T(8,128)(2,1)} %ri_ref.1, f32[1,256]{1,0:T(1,128)} %bitcast.2, s32[8192]{0:T(1024)} %order_ref.1), custom_call_target="tpu_custom_call" | custom-call | tf_op jit(solution)/shard_map/pallas_call | solution.py:336
  43.7 3.0 %collective-permute-start = (f32[1,1]{1,0:T(1,128)}, f32[1,1]{1,0:T(1,128)}, u32[]{:S(2)}, u32[]{:S(2)}) collective-permute-start(f32[1,1]{1,0:T(1,128)} %get-tuple-element.6), channel_id=1, source_target_pairs={{0,1},{1,0},{2,3},{3,2},{4,5},{5,4},{6,7},{7,6},{8,9},{9,8},{10,11... | collective-permute-start | bytes 20 | tf_op jit(solution)/shard_map/ppermute | solution.py:364
  46.7 2.3 %collective-permute-done = f32[1,1]{1,0:T(1,128)} collective-permute-done((f32[1,1]{1,0:T(1,128)}, f32[1,1]{1,0:T(1,128)}, u32[]{:S(2)}, u32[]{:S(2)}) %collective-permute-start) | collective-permute-done | bytes 36 | tf_op jit(solution)/shard_map/ppermute | solution.py:364
  50.3 1.9 %broadcast_multiply_fusion = (f32[256,256]{1,0:T(8,128)}, f32[256,256]{1,0:T(8,128)}) fusion(f32[256,256]{1,0:T(8,128)} %get-tuple-element.7, f32[]{:T(128)} %bitcast.1, f32[256,256]{1,0:T(8,128)} %get-tuple-element.5), kind=kLoop, calls=%fused_computation | loop fusion | flops 131072 | bytes 1048580 | tf_op jit(solution)/shard_map/mul | solution.py:366
Async XLA Ops:
  43.7 5.3 %collective-permute-start = (f32[1,1]{1,0:T(1,128)}, f32[1,1]{1,0:T(1,128)}, u32[]{:S(2)}, u32[]{:S(2)}) collective-permute-start(f32[1,1]{1,0:T(1,128)} %get-tuple-element.6), channel_id=1, source_target_pairs={{0,1},{1,0},{2,3},{3,2},{4,5},{5,4},{6,7},{7,6},{8,9},{9,8},{10,11... | collective-permute-start | bytes 20 | tf_op jit(solution)/shard_map/ppermute | solution.py:364

commit v4 on v3

--- a/solution.py
+++ b/solution.py
@@ -86,9 +86,9 @@
 
 
 def kernel(
-    devices,
+    devices, groups,
     lr_hbm, li_hbm, rr_ref, ri_ref, scale_ref, order_ref,
-    out_r, out_i, total_ref,
+    out_r, out_i, factor_ref,
     left_v, table, picked, perm, held, acc,
     left_sem, ring_send, ring_recv, pair_send, pair_recv,
     sums, sum_send, sum_recv,
@@ -102,6 +102,7 @@
     piece = 2 * cols // (2 * HALF)
 
     me = lax.axis_index("blk")
+    my_group = lax.axis_index("grp")
     chip, core = me // 2, lax.rem(me, 2)
     other = 1 - core
     z = lax.rem(chip, NZ)
@@ -139,13 +140,16 @@
     barrier = pltpu.get_barrier_semaphore()
     for target in (*ahead.values(), partner):
         pl.semaphore_signal(barrier, inc=1, device_id={"blk": target}, device_id_type=MESH)
+    for o in range(1, groups):
+        target = lax.rem(my_group + o, groups)
+        pl.semaphore_signal(barrier, inc=1, device_id={"grp": target}, device_id_type=MESH)
 
     for n, ref in enumerate((rr_ref, ri_ref)):
         held[me, n * cols:(n + 1) * cols, :] = (
             ref[...].astype(jnp.float32).T.astype(jnp.bfloat16)
         )
     acc[...] = jnp.zeros_like(acc)
-    pl.semaphore_wait(barrier, len(ahead) + 1)
+    pl.semaphore_wait(barrier, len(ahead) + groups)
 
     starts, events, moved = plan()
     slots = {}
@@ -285,8 +289,8 @@
         now += cost
     assert not todo
 
-    total_devices = devices
-    mine = me
+    total_devices = devices * groups
+    mine = my_group * devices + me
     low, high = pl.ds(0, cols), pl.ds(cols, cols)
     scale = scale_ref[...]
     real = (acc[low, 0:rows] - acc[high, rows:2 * rows]) * scale
@@ -300,7 +304,8 @@
         return pltpu.make_async_remote_copy(
             src_ref=sums.at[which], dst_ref=sums.at[which],
             send_sem=sum_send, recv_sem=sum_recv,
-            device_id={"blk": to}, device_id_type=MESH,
+            device_id={"blk": lax.rem(to, devices), "grp": to // devices},
+            device_id_type=MESH,
         )
 
     if DO_COMM:
@@ -320,7 +325,8 @@
             device_id={"blk": partner}, device_id_type=MESH,
         )
         exchange.wait_recv()
-    total_ref[...] = jnp.sum(jnp.sum(sums[...], axis=0), axis=1, keepdims=True)
+    total = jnp.sum(jnp.sum(sums[...], axis=0), axis=1, keepdims=True)
+    factor_ref[...] = 1.0 / jnp.sqrt(total / jnp.float32(rows * cols * total_devices))
     if DO_COMM:
         exchange.wait_send()
 
@@ -333,8 +339,8 @@
     far = pl.BlockSpec(memory_space=pl.ANY)
     words = 2 * rows // LANES
     out = jax.ShapeDtypeStruct((rows, cols), jnp.float32)
-    real, imag, total = pl.pallas_call(
-        functools.partial(kernel, devices),
+    real, imag, factor = pl.pallas_call(
+        functools.partial(kernel, devices, groups),
         out_shape=(out, out, jax.ShapeDtypeStruct((1, 1), jnp.float32)),
         in_specs=[far, far, vmem, vmem, vmem, pl.BlockSpec(memory_space=pltpu.SMEM)],
         out_specs=(vmem, vmem, vmem),
@@ -350,7 +356,7 @@
             pltpu.SemaphoreType.DMA((messages,)),
             pltpu.SemaphoreType.DMA,
             pltpu.SemaphoreType.DMA((8,)),
-            pltpu.VMEM((devices, 1, LANES), jnp.float32),
+            pltpu.VMEM((devices * groups, 1, LANES), jnp.float32),
             pltpu.SemaphoreType.DMA,
             pltpu.SemaphoreType.DMA,
         ],
@@ -358,11 +364,6 @@
             collective_id=0, has_side_effects=True, vmem_limit_bytes=60 * 1024 * 1024
         ),
     )(left_real, left_imag, right_real, right_imag, row_scale.reshape(1, rows), bond_order)
-    whole = total
-    for o in range(1, groups):
-        ring = [(g, (g + o) % groups) for g in range(groups)]
-        whole = whole + lax.ppermute(total, "grp", ring)
-    factor = 1.0 / jnp.sqrt(whole / jnp.float32(rows * cols * devices * groups))
     return real * factor, imag * factor
 
 

time: 52.3 us -> 48.9 us (0.935); the launches traced: 52.1 us -> 48 us
  starting transfers between devices: 2.98 us -> 0 us
  waiting for transfers between devices: 2.34 us -> 0 us
  Pallas kernels: 43.1 us -> 44.9 us
  between operations: 1.85 us -> 0.64 us
  other arithmetic: 1.86 us -> 2.49 us
    ppermute x1 -> x0, starting transfers between devices: 2.98 us -> none  [body(): whole = whole + lax.ppermute(total, 'grp', ring)]
    ppermute x1 -> x0, waiting for transfers between devices: 2.34 us -> none  [body(): whole = whole + lax.ppermute(total, 'grp', ring)]
    pallas_call x1, Pallas kernels: 43.1 us -> 44.9 us  [body(): pl.pallas_call(functools.partial(kernel, devices, groups), out_shape=(out...]
    mul x1, other arithmetic: 1.86 us -> 2.49 us  [body(): return (real * factor, imag * factor)]
  transfers between devices with their start and end apart: 1 -> 0, of which waited for: 1 -> 0; matrix products, arithmetic and copies ran while one was open for 0% -> 0% of each run, Pallas kernels for 0% -> 0%
where the time goes in v4:
time: 48.9 us; the launch traced here: 48 us
  Pallas kernels  44.9 us (92%)
  other arithmetic  2.49 us (5%)
  between operations  0.64 us (1%)
    pallas_call x1, Pallas kernels, body(): pl.pallas_call(functools.partial(kernel, devices, groups), out_shape=(out...  44.9 us
    mul x1, other arithmetic, body(): return (real * factor, imag * factor)  2.49 us

profile of v4, /device:TPU:0, one launch (start us, length us, event | category | flops | bytes accessed | tf_op | source)
XLA Modules:
  0.0 48.0 jit_solution(13487547325049763573)
XLA Ops:
  0.6 44.9 %shard_map.77 = (f32[256,256]{1,0:T(8,128)}, f32[256,256]{1,0:T(8,128)}, f32[1,1]{1,0:T(1,128)}) custom-call(bf16[256,8192]{1,0:T(8,128)(2,1)} %lr_hbm.1, bf16[256,8192]{1,0:T(8,128)(2,1)} %li_hbm.1, bf16[128,256]{1,0:T(8,128)(2,1)} %rr_ref.1, bf16[128,256]{1,0:T(8,128)(2,1)} %ri_ref.1, f32[1,256]{1,0:T(1,128)} %bitcast.2, s32[8192]{0:T(1024)} %order_ref.1), custom_call_target="tpu_custom_call" | custom-call | tf_op jit(solution)/shard_map/pallas_call | solution.py:342
  45.5 2.5 %broadcast_multiply_fusion = (f32[256,256]{1,0:T(8,128)}, f32[256,256]{1,0:T(8,128)}) fusion(f32[256,256]{1,0:T(8,128)} %get-tuple-element.7, f32[]{:T(128)} %bitcast.1, f32[256,256]{1,0:T(8,128)} %get-tuple-element.5), kind=kLoop, calls=%fused_computation | loop fusion | flops 131072 | bytes 1048580 | tf_op jit(solution)/shard_map/mul | solution.py:367
